TPU v7x, 8 devices: a whole 2x2x1 slice. The times are simulated.
8 devices in a mesh: dp: 1 (over z), pp: 8 (over y, x, core).
Axes of the slice: x: 2, y: 2, z: 1, core: 2. Of those that a mesh axis runs over, the one named last changes fastest.
Arguments:
- tokens: int32 [16, 2, 128], P('dp')
- targets: int32 [16, 2, 128], P('dp')
- emb: bfloat16 [49152, 2048], replicated
- g_final: bfloat16 [2048], replicated
- active: int32 [8, 1], P('pp')
- g_attn: bfloat16 [8, 1, 2048], P('pp')
- w_q: bfloat16 [8, 1, 2048, 2048], P('pp')
- w_k: bfloat16 [8, 1, 2048, 2048], P('pp')
- w_v: bfloat16 [8, 1, 2048, 2048], P('pp')
- w_o: bfloat16 [8, 1, 32, 64, 2048], P('pp')
- g_mlp: bfloat16 [8, 1, 2048], P('pp')
- w_gate: bfloat16 [8, 1, 2048, 8192], P('pp')
- w_up: bfloat16 [8, 1, 2048, 8192], P('pp')
- w_down: bfloat16 [8, 1, 8192, 2048], P('pp')
Outputs:
- output 1: float32 [16, 2, 128], P('dp')
- output 2: float32 [16], P('dp')
All inputs are finite; a program needn't handle non-finite values.
Results may differ from a plain program's by a relative error of at most 0.00352521.
Values are sent between devices in bfloat16 or wider.
A program may use at most 1.5 GiB of HBM per device.

v0:
```python
import functools
import math

import jax
import jax.numpy as jnp
from jax import lax
from jax.experimental import pallas as pl
from jax.experimental.pallas import tpu as pltpu
from jax.sharding import PartitionSpec as P

BF = jnp.bfloat16
F32 = jnp.float32
NORM_EPS = 1e-5
ROPE_BASE = 500000.0
ROPE_FACTOR = 32.0
ROPE_LOW = 1.0
ROPE_HIGH = 4.0
ROPE_ORIG = 8192.0

NMB = 16
ROWS = 256
D = 2048
FFN = 8192
VOCAB = 49152
CH = 512
NC = D // CH
NG = 3
BODIES = 17
FIRST, LAST = 1, 6
HG = 2048
HEAD_GROUPS = VOCAB // 2 // HG
FIN_GROUPS = VOCAB // 6 // HG
MESH = pl.DeviceIdType.MESH


def rope_tables():
    half = 32
    inv_freq = ROPE_BASE ** (-2.0 * jnp.arange(half, dtype=F32) / (2 * half))
    wavelen = 2.0 * math.pi / inv_freq
    smooth = jnp.clip((ROPE_ORIG / wavelen - ROPE_LOW) / (ROPE_HIGH - ROPE_LOW), 0.0, 1.0)
    scaled = (1.0 - smooth) * inv_freq / ROPE_FACTOR + smooth * inv_freq
    angles = jnp.arange(128, dtype=F32)[:, None] * scaled[None, :]
    c, s = jnp.cos(angles), jnp.sin(angles)
    z = jnp.zeros_like(s)
    cos = jnp.tile(c, (1, 4))
    sin_a = jnp.tile(jnp.concatenate([-s, z], 1), (1, 2))
    sin_b = jnp.tile(jnp.concatenate([z, s], 1), (1, 2))
    t = jnp.stack([cos, sin_a, sin_b])
    return jnp.concatenate([t * 0.125, t], 0)


def dotf(a, b):
    return jnp.dot(a, b, preferred_element_type=F32)


def dott(a, b):
    return lax.dot_general(a, b, (((1,), (1,)), ((), ())), preferred_element_type=F32)


def norm_rows(src, g_ref, dst):
    gains = [g_ref[:, CH * c:CH * (c + 1)].astype(F32) for c in range(NC)]

    def block(i, _):
        r0 = pl.multiple_of(i * 64, 64)
        for u in range(4):
            rows = pl.ds(r0 + 16 * u, 16)
            ss = None
            for c in range(NC):
                xv = src[c, rows, :].astype(F32)
                sq = xv * xv
                part = sq[:, :128] + sq[:, 128:256] + sq[:, 256:384] + sq[:, 384:]
                ss = part if ss is None else ss + part
            inv = lax.rsqrt(jnp.sum(ss, axis=1, keepdims=True) * (1.0 / D) + NORM_EPS)
            for c in range(NC):
                xv = src[c, rows, :].astype(F32)
                dst[rows, CH * c:CH * (c + 1)] = (xv * inv * gains[c]).astype(BF)
        return 0

    lax.fori_loop(0, ROWS // 64, block, 0)


def rope(y, tab, base):
    rows = []
    for s in range(2):
        cols = []
        for j in range(CH // 128):
            v = y[128 * s:128 * (s + 1), 128 * j:128 * (j + 1)]
            cols.append(v * tab[base] + pltpu.roll(v, 96, 1) * tab[base + 1] + pltpu.roll(v, 32, 1) * tab[base + 2])
        rows.append(jnp.concatenate(cols, axis=1))
    return jnp.concatenate(rows, axis=0)


def attend_probs(q, k, ch, pair, seq, lo, causal):
    rows, cols = pl.ds(128 * seq, 128), pl.ds(128 * pair, 128)
    qp, kp = q[ch, rows, cols], k[ch, rows, cols]
    zero = jnp.zeros((128, 128), BF)
    both = jnp.concatenate([jnp.where(lo, kp, zero), jnp.where(lo, zero, kp)], axis=0)
    scores = dott(qp, both)
    probs = []
    for head in range(2):
        z = jnp.where(causal, scores[:, 128 * head:128 * (head + 1)], -1e30)
        e = jnp.exp(z - jnp.max(z, axis=1, keepdims=True))
        probs.append((e * (1.0 / jnp.sum(e, axis=1, keepdims=True))).astype(BF))
    return jnp.concatenate(probs, axis=1)


def attend_values(q, v, ch, pair, seq, lo, probs):
    rows, cols = pl.ds(128 * seq, 128), pl.ds(128 * pair, 128)
    vp = v[ch, rows, cols]
    zero = jnp.zeros((128, 128), BF)
    both = jnp.concatenate([jnp.where(lo, vp, zero), jnp.where(lo, zero, vp)], axis=0)
    q[ch, rows, cols] = dotf(probs, both).astype(BF)


def kernel(x_hbm, emb, gf, tgt, ga, gm, wq, wk, wv, wo, wg, wu, wd, tab, flag, out,
           ring, res, xin, xfin, x1, h, q, k, v, a, xout, st, stf,
           wsem, rsem, xsem, recv_sem, send_sem, send0_sem, free_sem, free0_sem,
           fsend_sem, frecv_sem, ffwd_sem, ssend_sem, srecv_sem, tsend_sem, trecv_sem):
    me = lax.axis_index("pp")
    is_layer = jnp.logical_and(me >= FIRST, me <= LAST)
    is_head = jnp.logical_or(me == 0, me == 7)
    lane = lax.broadcasted_iota(jnp.int32, (128, 128), 1)
    lo = lane < 64
    causal = lax.broadcasted_iota(jnp.int32, (128, 128), 0) >= lane
    units = [(p, s) for p in range(4) for s in range(2)]

    def al(i, n):
        return i if isinstance(i, int) else pl.multiple_of(i, n)

    def slot_of(m, b):
        return lax.rem(BODIES * m + b, NG)

    def load(src, slot, t):
        pltpu.make_async_copy(src, ring.at[slot, t], wsem.at[slot]).start()

    def load_res(src, i):
        pltpu.make_async_copy(src, res.at[i], rsem.at[i]).start()

    def wait_group(slot):
        pltpu.make_async_copy(ring.at[slot], ring.at[slot], wsem.at[slot]).wait()

    def wait_res(i):
        pltpu.make_async_copy(res.at[i], res.at[i], rsem.at[i]).wait()

    def cols_of(w, c):
        return w.at[:, pl.ds(al(c * CH, CH), CH)]

    def start_qkv(i, slot):
        for t, w in enumerate((wq, wk, wv)):
            load(cols_of(w, i), slot, t)

    def start_out(slot):
        for t in range(3):
            load(cols_of(wo, t), slot, t)

    def start_ffn(c, slot):
        load(cols_of(wg, 2 * c), slot, 0)
        load(cols_of(wg, 2 * c + 1), slot, 1)
        load(cols_of(wu, 2 * c), slot, 2)

    def down_tile(n, t):
        return wd.at[pl.ds(D * t, D), pl.ds(al(n * CH, CH), CH)]

    def start_down(n, slot):
        for t in range(3):
            load(down_tile(n, t), slot, t)

    def to_next(s, n):
        return pltpu.make_async_remote_copy(xout.at[s, n], xin.at[s, n], send_sem.at[s, n], recv_sem.at[s, n],
                                            device_id={"pp": lax.rem(me + 1, 8)}, device_id_type=MESH)

    def to_zero(s, n):
        return pltpu.make_async_remote_copy(xout.at[s, n], xin.at[s, n], send0_sem.at[s, n], recv_sem.at[s, n],
                                            device_id={"pp": 0}, device_id_type=MESH)

    fin_targets = (7, 4, 2)

    def to_fin(i, s, n):
        return pltpu.make_async_remote_copy(xout.at[s, n], xfin.at[n], fsend_sem.at[i, n], frecv_sem.at[n],
                                            device_id={"pp": fin_targets[i]}, device_id_type=MESH)

    def forward(n):
        return pltpu.make_async_remote_copy(xfin.at[n], xfin.at[n], ffwd_sem.at[n], frecv_sem.at[n],
                                            device_id={"pp": lax.rem(me + 1, 8)}, device_id_type=MESH)

    def load_x(m, s, c):
        return pltpu.make_async_copy(x_hbm.at[m, :, pl.ds(CH * c, CH)], xin.at[s, c], xsem.at[s, c])

    def start_head(row, slot):
        for t in range(4):
            pltpu.make_async_copy(emb.at[pl.ds(al(row, HG), HG), pl.ds(CH * t, CH)], res.at[4 * slot + t], rsem.at[slot]).start()

    def wait_head(slot):
        view = res.at[pl.ds(4 * slot, 4)]
        pltpu.make_async_copy(view, view, rsem.at[slot]).wait()

    sub8 = lax.broadcasted_iota(jnp.int32, (8, ROWS), 0)

    def head_group(slot, row, y, carry):
        mx, sm, pk = carry
        yrel = y - row - sub8
        for nb in range(HG // CH):
            lg = None
            for t in range(4):
                part = dott(res[4 * slot + t, CH * nb:CH * (nb + 1), :], h[:, CH * t:CH * (t + 1)])
                lg = part if lg is None else lg + part
            l3 = lg.reshape(CH // 8, 8, ROWS)
            new = jnp.maximum(mx, jnp.max(l3, axis=0))
            sm = sm * jnp.exp(mx - new) + jnp.sum(jnp.exp(l3 - new[None]), axis=0)
            for r in range(CH // 8):
                pk = pk + jnp.where(yrel == CH * nb + 8 * r, l3[r], 0.0)
            mx = new
        return mx, sm, pk

    def head_start():
        return (jnp.full((8, ROWS), -3e38, F32), jnp.zeros((8, ROWS), F32), jnp.zeros((8, ROWS), F32))

    def head_stats(carry):
        mx, sm, pk = carry
        top = jnp.max(mx, axis=0, keepdims=True)
        tot = jnp.sum(sm * jnp.exp(mx - top), axis=0, keepdims=True)
        return top, tot, jnp.sum(pk, axis=0, keepdims=True)

    @pl.when(is_layer)
    def _():
        for i in range(3):
            start_qkv(i, i)

        @pl.when(me == FIRST)
        def _():
            for c in range(NC):
                load_x(0, 0, c).start()

        def one(m, _):
            s = lax.rem(m, 2)
            first = m == 0
            more = m < NMB - 1

            @pl.when(me == FIRST)
            def _():
                for c in range(NC):
                    load_x(m, s, c).wait()

                @pl.when(more)
                def _():
                    for c in range(NC):
                        load_x(m + 1, 1 - s, c).start()

            @pl.when(me != FIRST)
            def _():
                for c in range(NC):
                    to_next(s, c).wait_recv()

            norm_rows(xin.at[s], ga, h)
            on = flag[0:1, 0:1] != 0

            def qkv(i, prev):
                slot = slot_of(m, i)
                wait_group(slot)
                plan = [units[:4], units[4:], []] if prev is not None else [[], [], []]
                for j, dst in enumerate((q, k, v)):
                    ps = [attend_probs(q, k, prev, p, sq, lo, causal) for p, sq in plan[j]]
                    r = dotf(h[...], ring[slot, j])
                    if j < 2:
                        r = rope(r, tab, 3 * j)
                    dst[i] = r.astype(BF)
                    for (p, sq), pr in zip(plan[j], ps):
                        attend_values(q, v, prev, p, sq, lo, pr)
                return slot

            slot = qkv(0, None)
            start_qkv(3, slot)

            def qkv_loop(i, _):
                slot = qkv(i, i - 1)

                @pl.when(i == 1)
                def _():
                    start_out(slot)

                    @pl.when(first)
                    def _():
                        load_res(cols_of(wo, 3), 0)

                @pl.when(i > 1)
                def _():
                    start_ffn(i - 2, slot)

                    @pl.when(first)
                    def _():
                        load_res(cols_of(wu, 2 * (i - 2) + 1), 1 + i - 2)
                return 0

            lax.fori_loop(1, 4, qkv_loop, 0)
            ps = [attend_probs(q, k, 3, p, sq, lo, causal) for p, sq in units]
            for (p, sq), pr in zip(units, ps):
                attend_values(q, v, 3, p, sq, lo, pr)

            slot = slot_of(m, 4)
            wait_group(slot)

            @pl.when(first)
            def _():
                wait_res(0)

            for t in range(4):
                w = ring.at[slot, t] if t < 3 else res.at[0]
                r = None
                for kc in range(NC):
                    part = dotf(q[kc], w[CH * kc:CH * (kc + 1), :])
                    r = part if r is None else r + part
                xo = xin[s, t]
                x1[t] = jnp.where(on, (xo.astype(F32) + r).astype(BF), xo)
            start_ffn(2, slot)

            @pl.when(first)
            def _():
                load_res(cols_of(wu, 2 * 2 + 1), 1 + 2)

            @pl.when(jnp.logical_and(me != FIRST, m < NMB - 2))
            def _():
                pl.semaphore_signal(free_sem, 1, device_id={"pp": lax.rem(me + 7, 8)}, device_id_type=MESH)

            norm_rows(x1, gm, h)

            def ffn(c, _):
                slot = slot_of(m, 5 + c)
                wait_group(slot)

                @pl.when(first)
                def _():
                    wait_res(1 + c)

                for t in range(2):
                    gate = dotf(h[...], ring[slot, t])
                    up = dotf(h[...], ring[slot, 2] if t == 0 else res[1 + c])
                    a[c, :, CH * t:CH * (t + 1)] = (gate * (1.0 / (1.0 + jnp.exp(-gate))) * up).astype(BF)

                @pl.when(c < 5)
                def _():
                    start_ffn(c + 3, slot)

                    @pl.when(first)
                    def _():
                        load_res(cols_of(wu, 2 * (c + 3) + 1), 1 + c + 3)

                @pl.when(c >= 5)
                def _():
                    start_down(c - 5, slot)

                    @pl.when(first)
                    def _():
                        load_res(down_tile(c - 5, 3), 9 + c - 5)
                return 0

            lax.fori_loop(0, 8, ffn, 0)

            @pl.when(jnp.logical_and(m >= 2, jnp.logical_or(more, me != LAST)))
            def _():
                pl.semaphore_wait(free_sem, 1)

                @pl.when(me == LAST)
                def _():
                    pl.semaphore_wait(free0_sem, 1)

            def down(n, _):
                slot = slot_of(m, 13 + n)
                wait_group(slot)

                @pl.when(first)
                def _():
                    wait_res(9 + n)

                @pl.when(m >= 2)
                def _():
                    to_next(s, n).wait_send()

                    @pl.when(me == LAST)
                    def _():
                        to_zero(s, n).wait_send()

                acc = None
                for t in range(4):
                    w = ring.at[slot, t] if t < 3 else res.at[9 + n]
                    for u in range(2):
                        part = dotf(a[2 * t + u], w[1024 * u:1024 * (u + 1), :])
                        acc = part if acc is None else acc + part
                xo = x1[n]
                xout[s, n] = jnp.where(on, (xo.astype(F32) + acc).astype(BF), xo)

                @pl.when(jnp.logical_or(more, me != LAST))
                def _():
                    to_next(s, n).start()

                @pl.when(me == LAST)
                def _():
                    @pl.when(more)
                    def _():
                        to_zero(s, n).start()

                    @pl.when(jnp.logical_not(more))
                    def _():
                        for i in range(3):
                            to_fin(i, s, n).start()

                @pl.when(n == 0)
                def _():
                    start_down(3, slot)

                    @pl.when(first)
                    def _():
                        load_res(down_tile(3, 3), 12)

                @pl.when(jnp.logical_and(n > 0, more))
                def _():
                    start_qkv(n - 1, slot)
                return 0

            lax.fori_loop(0, NC, down, 0)
            return 0

        lax.fori_loop(0, NMB, one, 0)

    side = jnp.where(me == 7, 1, 0)
    base = side * (VOCAB // 2)

    def stats_to(i):
        return pltpu.make_async_remote_copy(st.at[side], st.at[side], ssend_sem.at[i], srecv_sem.at[side],
                                            device_id={"pp": lax.rem(me + 1 + i, 8)}, device_id_type=MESH)

    @pl.when(is_head)
    def _():
        for g in range(3):
            start_head(base + HG * g, g)

        def one(m, _):
            s = lax.rem(m, 2)
            for c in range(NC):
                to_next(s, c).wait_recv()
            norm_rows(xin.at[s], gf, h)

            @pl.when(m < NMB - 3)
            def _():
                @pl.when(me == 7)
                def _():
                    pl.semaphore_signal(free_sem, 1, device_id={"pp": LAST}, device_id_type=MESH)

                @pl.when(me == 0)
                def _():
                    pl.semaphore_signal(free0_sem, 1, device_id={"pp": LAST}, device_id_type=MESH)

            y = tgt[pl.ds(m, 1), :]

            def group(g, carry):
                slot = lax.rem(g, 3)
                wait_head(slot)
                row = base + HG * g
                carry = head_group(slot, row, y, carry)

                @pl.when(g < HEAD_GROUPS - 3)
                def _():
                    start_head(row + 3 * HG, slot)

                @pl.when(jnp.logical_and(g >= HEAD_GROUPS - 3, m < NMB - 2))
                def _():
                    start_head(row + 3 * HG - HG * HEAD_GROUPS, slot)
                return carry

            top, tot, pick = head_stats(lax.fori_loop(0, HEAD_GROUPS, group, head_start()))
            st[side, 0, pl.ds(m, 1), :] = top
            st[side, 1, pl.ds(m, 1), :] = tot
            st[side, 2, pl.ds(m, 1), :] = pick
            return 0

        lax.fori_loop(0, NMB - 1, one, 0)
        for j in range(3):
            st[side, j, NMB - 1:NMB, :] = jnp.ones((1, ROWS), F32)
        for i in range(7):
            stats_to(i).start()

    part = me - 2

    def fin_to(i):
        return pltpu.make_async_remote_copy(stf.at[part], stf.at[part], tsend_sem.at[i], trecv_sem.at[part],
                                            device_id={"pp": lax.rem(me + 1 + i, 8)}, device_id_type=MESH)

    @pl.when(me >= 2)
    def _():
        row0 = part * (HG * FIN_GROUPS)
        for g in range(3):
            start_head(row0 + HG * g, g)

        @pl.when(me == LAST)
        def _():
            for n in range(NC):
                xfin[n] = xout[(NMB - 1) % 2, n]

        @pl.when(me != LAST)
        def _():
            for n in range(NC):
                forward(n).wait_recv()

                @pl.when(jnp.logical_or(me == 2, me == 4))
                def _():
                    forward(n).start()

        norm_rows(xfin, gf, h)
        y = tgt[NMB - 1:NMB, :]

        def group(g, carry):
            slot = lax.rem(g, 3)
            wait_head(slot)
            row = row0 + HG * g
            carry = head_group(slot, row, y, carry)

            @pl.when(g < FIN_GROUPS - 3)
            def _():
                start_head(row + 3 * HG, slot)
            return carry

        top, tot, pick = head_stats(lax.fori_loop(0, FIN_GROUPS, group, head_start()))
        stf[part] = jnp.concatenate([top, tot, pick, jnp.zeros((5, ROWS), F32)], axis=0)
        for i in range(7):
            fin_to(i).start()

    for d in range(2):
        @pl.when(me != 7 * d)
        def _():
            pltpu.make_async_copy(st.at[d], st.at[d], srecv_sem.at[d]).wait()
    for f in range(6):
        @pl.when(me != f + 2)
        def _():
            pltpu.make_async_copy(stf.at[f], stf.at[f], trecv_sem.at[f]).wait()

    top = jnp.maximum(st[0, 0], st[1, 0])
    tot = st[0, 1] * jnp.exp(st[0, 0] - top) + st[1, 1] * jnp.exp(st[1, 0] - top)
    out[...] = jnp.log(tot) + top - (st[0, 2] + st[1, 2])
    ftop = stf[0, 0:1, :]
    for f in range(1, 6):
        ftop = jnp.maximum(ftop, stf[f, 0:1, :])
    ftot = jnp.zeros((1, ROWS), F32)
    fpick = jnp.zeros((1, ROWS), F32)
    for f in range(6):
        ftot = ftot + stf[f, 1:2, :] * jnp.exp(stf[f, 0:1, :] - ftop)
        fpick = fpick + stf[f, 2:3, :]
    out[NMB - 1:NMB, :] = jnp.log(ftot) + ftop - fpick

    @pl.when(is_layer)
    def _():
        for n in range(NC):
            to_next(0, n).wait_send()

            @pl.when(me != LAST)
            def _():
                to_next(1, n).wait_send()

            @pl.when(me == LAST)
            def _():
                to_zero(0, n).wait_send()
                for i in range(3):
                    to_fin(i, 1, n).wait_send()

    @pl.when(is_head)
    def _():
        for i in range(7):
            stats_to(i).wait_send()

    @pl.when(me >= 2)
    def _():
        for i in range(7):
            fin_to(i).wait_send()

        @pl.when(jnp.logical_or(me == 2, me == 4))
        def _():
            for n in range(NC):
                forward(n).wait_send()


def solution(mesh):
    def stage_program(tokens, targets, emb, g_final, active, g_attn, w_q, w_k, w_v, w_o, g_mlp, w_gate, w_up, w_down):
        x = jnp.take(emb, tokens.reshape(NMB * ROWS), axis=0).reshape(NMB, ROWS, D)
        flag = jnp.broadcast_to(active.reshape(1, 1), (8, 128))
        hbm = pl.BlockSpec(memory_space=pltpu.HBM)
        vmem = pl.BlockSpec(memory_space=pltpu.VMEM)
        dma, regular = pltpu.SemaphoreType.DMA, pltpu.SemaphoreType.REGULAR
        token_loss = pl.pallas_call(
            kernel,
            out_shape=jax.ShapeDtypeStruct((NMB, ROWS), F32),
            in_specs=[hbm, hbm, vmem, vmem, vmem, vmem] + [hbm] * 7 + [vmem, vmem],
            out_specs=vmem,
            scratch_shapes=[
                pltpu.VMEM((NG, 3, D, CH), BF),
                pltpu.VMEM((13, D, CH), BF),
                pltpu.VMEM((2, NC, ROWS, CH), BF),
                pltpu.VMEM((NC, ROWS, CH), BF),
                pltpu.VMEM((NC, ROWS, CH), BF),
                pltpu.VMEM((ROWS, D), BF),
                pltpu.VMEM((NC, ROWS, CH), BF),
                pltpu.VMEM((NC, ROWS, CH), BF),
                pltpu.VMEM((NC, ROWS, CH), BF),
                pltpu.VMEM((8, ROWS, 1024), BF),
                pltpu.VMEM((2, NC, ROWS, CH), BF),
                pltpu.VMEM((2, 3, NMB, ROWS), F32),
                pltpu.VMEM((6, 8, ROWS), F32),
                dma((NG,)), dma((13,)), dma((2, NC)), dma((2, NC)), dma((2, NC)), dma((2, NC)), regular, regular,
                dma((3, NC)), dma((NC,)), dma((NC,)), dma((7,)), dma((2,)), dma((7,)), dma((6,)),
            ],
            compiler_params=pltpu.CompilerParams(vmem_limit_bytes=67043328, has_side_effects=True),
        )(x, emb, g_final.reshape(1, D), targets.reshape(NMB, ROWS), g_attn.reshape(1, D), g_mlp.reshape(1, D),
          w_q.reshape(D, D), w_k.reshape(D, D), w_v.reshape(D, D), w_o.reshape(D, D),
          w_gate.reshape(D, FFN), w_up.reshape(D, FFN), w_down.reshape(FFN, D), rope_tables(), flag)
        return token_loss.reshape(NMB, 2, 128), jnp.mean(token_loss, axis=1)

    stack = P("pp")
    in_specs = (P("dp"), P("dp"), P(), P()) + (stack,) * 10
    return jax.shard_map(stage_program, mesh=mesh, in_specs=in_specs, out_specs=(P("dp"), P("dp")), check_vma=False)
```

profile of v0, /device:TPU:0, one launch (start us, length us, event | category | flops | bytes accessed | tf_op | source)
XLA Modules:
  0.0 1057.3 jit_solution(17384427481361395468)
XLA Ops:
  0.6 0.7 compare_select_fusion
  1.4 0.0 copy-start
  1.4 95.7 %gather_fusion = bf16[4096,2048]{1,0:T(8,128)(2,1)} fusion(bf16[49152,2048]{1,0:T(8,128)(2,1)} %emb.1, s32[4096]{0:T(1024)S(1)} %broadcast_clamp_fusion), kind=kCustom, calls=%fused_computation | custom fusion | bytes 33570816 | tf_op jit(solution)/shard_map/jit(_take)/gather | solution.py:581
  97.1 0.0 copy-done
  97.1 0.0 copy-start.2
  97.2 0.0 copy-start.1
  97.2 14.2 %broadcast_select_fusion.x_hbm = bf16[16,256,2048]{2,1,0:T(8,128)(2,1)} fusion(bf16[16,256,2048]{2,1,0:T(8,128)(2,1)} %bitcast.26, pred[16,256]{1,0:T(8,128)(4,1)S(1)} %compare_and_fusion), kind=kLoop, calls=%fused_computation.1 | loop fusion | flops 8388608 | bytes 33558528 | tf_op jit(solution)/shard_map/jit(_take)/select_n | solution.py:581
  111.3 0.0 copy-done.2
  111.3 0.6 reshape.143.gf
  111.9 0.0 copy-done.1
  111.9 0.6 copy.28
  112.6 0.1 fusion.1
  112.7 0.1 copy.18
  112.9 0.1 copy.17
  113.0 0.1 copy.16
  113.1 0.8 pad_maximum_fusion.tab
  114.5 0.6 broadcast_in_dim.23.flag
  115.1 939.5 %shard_map.149 = f32[16,256]{1,0:T(8,128)} custom-call(bf16[16,256,2048]{2,1,0:T(8,128)(2,1)} %broadcast_select_fusion.x_hbm, bf16[49152,2048]{1,0:T(8,128)(2,1)} %emb.1, bf16[1,2048]{1,0:T(2,128)(2,1)} %reshape.143.gf, s32[16,256]{1,0:T(8,128)} %bitcast.37, bf16[1,2048]{1,0:T(2,128)(2,1)} %bitcast.42, bf16[1,2048]{1,0:T(2,128)(2,1)} %bitcast.43, ...), custom_call_target="tpu_custom_call" | custom-call | tf_op jit(solution)/shard_map/pallas_call | solution.py:586
  1054.6 1.3 reshape.154
  1055.9 0.8 reduce_sum.9
  1056.8 0.5 broadcast_multiply_fusion
  (9 shorter events, 0.1 us)
Async XLA Ops:
  1.4 95.8 %copy-start = (s32[16,2,128]{2,1,0:T(2,128)S(1)}, s32[16,2,128]{2,1,0:T(2,128)}, u32[]{:S(2)}) copy-start(s32[16,2,128]{2,1,0:T(2,128)} %param.14) | copy-start | bytes 49156
  97.1 14.2 %copy-start.2 = (bf16[2048]{0:T(1024)(128)(2,1)S(1)}, bf16[2048]{0:T(1024)(128)(2,1)}, u32[]{:S(2)}) copy-start(bf16[2048]{0:T(1024)(128)(2,1)} %param.17) | copy-start | bytes 12292
  97.2 14.8 %copy-start.1 = (s32[16,2,128]{2,1,0:T(2,128)S(1)}, s32[16,2,128]{2,1,0:T(2,128)}, u32[]{:S(2)}) copy-start(s32[16,2,128]{2,1,0:T(2,128)} %param.15) | copy-start | bytes 49156
where the time goes:
time: 1060 us
  Pallas kernels  939 us (89%)
  local copies, waits for them, and re-layouts  99.2 us (9%)
  other arithmetic  17.2 us (2%)
    pallas_call x1, Pallas kernels, stage_program(): pl.pallas_call(kernel, out_shape=jax.ShapeDtypeStruct((NMB, ROWS), F32),...  939 us
    gather x1, local copies, waits for them, and re-layouts, stage_program(): x = jnp.take(emb, tokens.reshape(NMB * ROWS), axis=0).reshape(NMB, ROWS, D)  95.7 us

commit v1 on v0

--- a/solution.py
+++ b/solution.py
@@ -3,6 +3,7 @@
 
 import jax
 import jax.numpy as jnp
+import numpy as np
 from jax import lax
 from jax.experimental import pallas as pl
 from jax.experimental.pallas import tpu as pltpu
@@ -35,18 +36,15 @@
 
 def rope_tables():
     half = 32
-    inv_freq = ROPE_BASE ** (-2.0 * jnp.arange(half, dtype=F32) / (2 * half))
+    inv_freq = ROPE_BASE ** (-2.0 * np.arange(half) / (2 * half))
     wavelen = 2.0 * math.pi / inv_freq
-    smooth = jnp.clip((ROPE_ORIG / wavelen - ROPE_LOW) / (ROPE_HIGH - ROPE_LOW), 0.0, 1.0)
+    smooth = np.clip((ROPE_ORIG / wavelen - ROPE_LOW) / (ROPE_HIGH - ROPE_LOW), 0.0, 1.0)
     scaled = (1.0 - smooth) * inv_freq / ROPE_FACTOR + smooth * inv_freq
-    angles = jnp.arange(128, dtype=F32)[:, None] * scaled[None, :]
-    c, s = jnp.cos(angles), jnp.sin(angles)
-    z = jnp.zeros_like(s)
-    cos = jnp.tile(c, (1, 4))
-    sin_a = jnp.tile(jnp.concatenate([-s, z], 1), (1, 2))
-    sin_b = jnp.tile(jnp.concatenate([z, s], 1), (1, 2))
-    t = jnp.stack([cos, sin_a, sin_b])
-    return jnp.concatenate([t * 0.125, t], 0)
+    angles = np.arange(128)[:, None] * scaled[None, :]
+    c, s = np.cos(angles), np.sin(angles)
+    z = np.zeros_like(s)
+    t = np.stack([np.tile(c, (1, 4)), np.tile(np.concatenate([-s, z], 1), (1, 2)), np.tile(np.concatenate([z, s], 1), (1, 2))])
+    return np.concatenate([t * 0.125, t], 0).astype(np.float32)
 
 
 def dotf(a, b):
@@ -61,8 +59,8 @@
     gains = [g_ref[:, CH * c:CH * (c + 1)].astype(F32) for c in range(NC)]
 
     def block(i, _):
-        r0 = pl.multiple_of(i * 64, 64)
-        for u in range(4):
+        r0 = pl.multiple_of(i * 128, 128)
+        for u in range(8):
             rows = pl.ds(r0 + 16 * u, 16)
             ss = None
             for c in range(NC):
@@ -76,7 +74,7 @@
                 dst[rows, CH * c:CH * (c + 1)] = (xv * inv * gains[c]).astype(BF)
         return 0
 
-    lax.fori_loop(0, ROWS // 64, block, 0)
+    lax.fori_loop(0, ROWS // 128, block, 0)
 
 
 def rope(y, tab, base):
@@ -112,10 +110,10 @@
     q[ch, rows, cols] = dotf(probs, both).astype(BF)
 
 
-def kernel(x_hbm, emb, gf, tgt, ga, gm, wq, wk, wv, wo, wg, wu, wd, tab, flag, out,
+def kernel(x_hbm, emb, gf, tgt, ga, gm, wq, wk, wv, wo, wg, wu, wd, tab, flag, out, out_mean, xbuf,
            ring, res, xin, xfin, x1, h, q, k, v, a, xout, st, stf,
            wsem, rsem, xsem, recv_sem, send_sem, send0_sem, free_sem, free0_sem,
-           fsend_sem, frecv_sem, ffwd_sem, ssend_sem, srecv_sem, tsend_sem, trecv_sem):
+           fsend_sem, frecv_sem, ffwd_sem, ssend_sem, srecv_sem, tsend_sem, trecv_sem, gsend_sem, grecv_sem):
     me = lax.axis_index("pp")
     is_layer = jnp.logical_and(me >= FIRST, me <= LAST)
     is_head = jnp.logical_or(me == 0, me == 7)
@@ -183,8 +181,33 @@
         return pltpu.make_async_remote_copy(xfin.at[n], xfin.at[n], ffwd_sem.at[n], frecv_sem.at[n],
                                             device_id={"pp": lax.rem(me + 1, 8)}, device_id_type=MESH)
 
-    def load_x(m, s, c):
-        return pltpu.make_async_copy(x_hbm.at[m, :, pl.ds(CH * c, CH)], xin.at[s, c], xsem.at[s, c])
+    pair = jnp.where(me == 0, 1, me)
+
+    def to_first():
+        return pltpu.make_async_remote_copy(x_hbm, xbuf.at[pair], gsend_sem, grecv_sem.at[pair],
+                                            device_id={"pp": FIRST}, device_id_type=MESH)
+
+    def start_x(m, s):
+        cols = [pl.ds(CH * c, CH) for c in range(NC)]
+
+        @pl.when(m < 2)
+        def _():
+            for c in range(NC):
+                pltpu.make_async_copy(x_hbm.at[m, :, cols[c]], xin.at[s, c], xsem.at[s]).start()
+
+        @pl.when(m >= 2)
+        def _():
+            p = m // 2
+
+            @pl.when(m == 2 * p)
+            def _():
+                pltpu.make_async_copy(xbuf.at[p], xbuf.at[p], grecv_sem.at[p]).wait()
+
+            for c in range(NC):
+                pltpu.make_async_copy(xbuf.at[p, m - 2 * p, :, cols[c]], xin.at[s, c], xsem.at[s]).start()
+
+    def wait_x(s):
+        pltpu.make_async_copy(xin.at[s], xin.at[s], xsem.at[s]).wait()
 
     def start_head(row, slot):
         for t in range(4):
@@ -221,30 +244,40 @@
         tot = jnp.sum(sm * jnp.exp(mx - top), axis=0, keepdims=True)
         return top, tot, jnp.sum(pk, axis=0, keepdims=True)
 
+    @pl.when(me != FIRST)
+    def _():
+        to_first().start()
+
     @pl.when(is_layer)
     def _():
+        @pl.when(me == FIRST)
+        def _():
+            start_x(0, 0)
+
         for i in range(3):
             start_qkv(i, i)
 
-        @pl.when(me == FIRST)
-        def _():
-            for c in range(NC):
-                load_x(0, 0, c).start()
+        @pl.when(me != FIRST)
+        def _():
+            load_res(cols_of(wo, 3), 0)
+            for c in range(8):
+                load_res(cols_of(wu, 2 * c + 1), 1 + c)
+            for n in range(NC):
+                load_res(down_tile(n, 3), 9 + n)
 
         def one(m, _):
             s = lax.rem(m, 2)
             first = m == 0
+            fresh = jnp.logical_and(first, me == FIRST)
             more = m < NMB - 1
 
             @pl.when(me == FIRST)
             def _():
-                for c in range(NC):
-                    load_x(m, s, c).wait()
+                wait_x(s)
 
                 @pl.when(more)
                 def _():
-                    for c in range(NC):
-                        load_x(m + 1, 1 - s, c).start()
+                    start_x(m + 1, 1 - s)
 
             @pl.when(me != FIRST)
             def _():
@@ -257,20 +290,35 @@
             def qkv(i, prev):
                 slot = slot_of(m, i)
                 wait_group(slot)
-                plan = [units[:4], units[4:], []] if prev is not None else [[], [], []]
+                us = units if prev is not None else []
+                ps = [attend_probs(q, k, prev, p, sq, lo, causal) for p, sq in us]
                 for j, dst in enumerate((q, k, v)):
-                    ps = [attend_probs(q, k, prev, p, sq, lo, causal) for p, sq in plan[j]]
                     r = dotf(h[...], ring[slot, j])
                     if j < 2:
                         r = rope(r, tab, 3 * j)
                     dst[i] = r.astype(BF)
-                    for (p, sq), pr in zip(plan[j], ps):
+                    for (p, sq), pr in zip(us, ps) if j == 1 else ():
                         attend_values(q, v, prev, p, sq, lo, pr)
                 return slot
 
             slot = qkv(0, None)
             start_qkv(3, slot)
 
+            def qkv_static(i):
+                slot = qkv(i, i - 1)
+                if i == 1:
+                    start_out(slot)
+
+                    @pl.when(fresh)
+                    def _():
+                        load_res(cols_of(wo, 3), 0)
+                else:
+                    start_ffn(i - 2, slot)
+
+                    @pl.when(fresh)
+                    def _():
+                        load_res(cols_of(wu, 2 * (i - 2) + 1), 1 + i - 2)
+
             def qkv_loop(i, _):
                 slot = qkv(i, i - 1)
 
@@ -278,7 +326,7 @@
                 def _():
                     start_out(slot)
 
-                    @pl.when(first)
+                    @pl.when(fresh)
                     def _():
                         load_res(cols_of(wo, 3), 0)
 
@@ -286,34 +334,42 @@
                 def _():
                     start_ffn(i - 2, slot)
 
-                    @pl.when(first)
+                    @pl.when(fresh)
                     def _():
                         load_res(cols_of(wu, 2 * (i - 2) + 1), 1 + i - 2)
                 return 0
 
-            lax.fori_loop(1, 4, qkv_loop, 0)
+            for i in range(1, 4):
+                qkv_static(i)
+            slot = slot_of(m, 4)
+            wait_group(slot)
+
+            @pl.when(first)
+            def _():
+                wait_res(0)
+
+            def out_tile(t):
+                return ring.at[slot, t] if t < 3 else res.at[0]
+
+            def out_part(t):
+                w, r = out_tile(t), None
+                for kc in range(NC - 1):
+                    part = dotf(q[kc], w[CH * kc:CH * (kc + 1), :])
+                    r = part if r is None else r + part
+                return r
+
             ps = [attend_probs(q, k, 3, p, sq, lo, causal) for p, sq in units]
+            done = [out_part(t) for t in range(2)]
             for (p, sq), pr in zip(units, ps):
                 attend_values(q, v, 3, p, sq, lo, pr)
-
-            slot = slot_of(m, 4)
-            wait_group(slot)
-
-            @pl.when(first)
-            def _():
-                wait_res(0)
-
-            for t in range(4):
-                w = ring.at[slot, t] if t < 3 else res.at[0]
-                r = None
-                for kc in range(NC):
-                    part = dotf(q[kc], w[CH * kc:CH * (kc + 1), :])
-                    r = part if r is None else r + part
+            done += [out_part(t) for t in range(2, NC)]
+            for t in range(NC):
+                r = done[t] + dotf(q[3], out_tile(t)[CH * 3:, :])
                 xo = xin[s, t]
                 x1[t] = jnp.where(on, (xo.astype(F32) + r).astype(BF), xo)
             start_ffn(2, slot)
 
-            @pl.when(first)
+            @pl.when(fresh)
             def _():
                 load_res(cols_of(wu, 2 * 2 + 1), 1 + 2)
 
@@ -322,6 +378,11 @@
                 pl.semaphore_signal(free_sem, 1, device_id={"pp": lax.rem(me + 7, 8)}, device_id_type=MESH)
 
             norm_rows(x1, gm, h)
+
+            def ffn2(i, _):
+                for e in range(4):
+                    ffn(4 * i + e, 0)
+                return 0
 
             def ffn(c, _):
                 slot = slot_of(m, 5 + c)
@@ -340,7 +401,7 @@
                 def _():
                     start_ffn(c + 3, slot)
 
-                    @pl.when(first)
+                    @pl.when(fresh)
                     def _():
                         load_res(cols_of(wu, 2 * (c + 3) + 1), 1 + c + 3)
 
@@ -348,12 +409,12 @@
                 def _():
                     start_down(c - 5, slot)
 
-                    @pl.when(first)
+                    @pl.when(fresh)
                     def _():
                         load_res(down_tile(c - 5, 3), 9 + c - 5)
                 return 0
 
-            lax.fori_loop(0, 8, ffn, 0)
+            lax.fori_loop(0, 2, ffn2, 0)
 
             @pl.when(jnp.logical_and(m >= 2, jnp.logical_or(more, me != LAST)))
             def _():
@@ -403,20 +464,20 @@
                         for i in range(3):
                             to_fin(i, s, n).start()
 
-                @pl.when(n == 0)
-                def _():
+                if n == 0:
                     start_down(3, slot)
 
-                    @pl.when(first)
+                    @pl.when(fresh)
                     def _():
                         load_res(down_tile(3, 3), 12)
-
-                @pl.when(jnp.logical_and(n > 0, more))
-                def _():
-                    start_qkv(n - 1, slot)
+                else:
+                    @pl.when(more)
+                    def _():
+                        start_qkv(n - 1, slot)
                 return 0
 
-            lax.fori_loop(0, NC, down, 0)
+            for n in range(NC):
+                down(n, 0)
             return 0
 
         lax.fori_loop(0, NMB, one, 0)
@@ -534,7 +595,7 @@
 
     top = jnp.maximum(st[0, 0], st[1, 0])
     tot = st[0, 1] * jnp.exp(st[0, 0] - top) + st[1, 1] * jnp.exp(st[1, 0] - top)
-    out[...] = jnp.log(tot) + top - (st[0, 2] + st[1, 2])
+    loss = jnp.log(tot) + top - (st[0, 2] + st[1, 2])
     ftop = stf[0, 0:1, :]
     for f in range(1, 6):
         ftop = jnp.maximum(ftop, stf[f, 0:1, :])
@@ -543,7 +604,17 @@
     for f in range(6):
         ftot = ftot + stf[f, 1:2, :] * jnp.exp(stf[f, 0:1, :] - ftop)
         fpick = fpick + stf[f, 2:3, :]
-    out[NMB - 1:NMB, :] = jnp.log(ftot) + ftop - fpick
+    last = lax.broadcasted_iota(jnp.int32, (NMB, ROWS), 0) == NMB - 1
+    loss = jnp.where(last, jnp.log(ftot) + ftop - fpick, loss)
+    out[:, 0, :] = loss[:, :128]
+    out[:, 1, :] = loss[:, 128:]
+    mean = jnp.sum(loss, axis=1, keepdims=True) * (1.0 / ROWS)
+    here = lax.broadcasted_iota(jnp.int32, (NMB, 128), 0) == lax.broadcasted_iota(jnp.int32, (NMB, 128), 1)
+    out_mean[...] = jnp.sum(jnp.where(here, mean, 0.0), axis=0, keepdims=True)
+
+    @pl.when(me != FIRST)
+    def _():
+        to_first().wait_send()
 
     @pl.when(is_layer)
     def _():
@@ -576,40 +647,48 @@
                 forward(n).wait_send()
 
 
+def run_kernel(*args):
+    hbm = pl.BlockSpec(memory_space=pltpu.HBM)
+    vmem = pl.BlockSpec(memory_space=pltpu.VMEM)
+    dma, regular = pltpu.SemaphoreType.DMA, pltpu.SemaphoreType.REGULAR
+    return pl.pallas_call(
+        kernel,
+        out_shape=(jax.ShapeDtypeStruct((NMB, 2, 128), F32), jax.ShapeDtypeStruct((1, 128), F32),
+                   jax.ShapeDtypeStruct((NMB // 2, 2, ROWS, D), BF)),
+        in_specs=[hbm, hbm, vmem, vmem, vmem, vmem] + [hbm] * 7 + [vmem, vmem],
+        out_specs=(vmem, vmem, hbm),
+        scratch_shapes=[
+            pltpu.VMEM((NG, 3, D, CH), BF),
+            pltpu.VMEM((13, D, CH), BF),
+            pltpu.VMEM((2, NC, ROWS, CH), BF),
+            pltpu.VMEM((NC, ROWS, CH), BF),
+            pltpu.VMEM((NC, ROWS, CH), BF),
+            pltpu.VMEM((ROWS, D), BF),
+            pltpu.VMEM((NC, ROWS, CH), BF),
+            pltpu.VMEM((NC, ROWS, CH), BF),
+            pltpu.VMEM((NC, ROWS, CH), BF),
+            pltpu.VMEM((8, ROWS, 1024), BF),
+            pltpu.VMEM((2, NC, ROWS, CH), BF),
+            pltpu.VMEM((2, 3, NMB, ROWS), F32),
+            pltpu.VMEM((6, 8, ROWS), F32),
+            dma((NG,)), dma((13,)), dma((2,)), dma((2, NC)), dma((2, NC)), dma((2, NC)), regular, regular,
+            dma((3, NC)), dma((NC,)), dma((NC,)), dma((7,)), dma((2,)), dma((7,)), dma((6,)), dma(()), dma((8,)),
+        ],
+        compiler_params=pltpu.CompilerParams(vmem_limit_bytes=67043328, has_side_effects=True),
+    )(*args)
+
+
 def solution(mesh):
     def stage_program(tokens, targets, emb, g_final, active, g_attn, w_q, w_k, w_v, w_o, g_mlp, w_gate, w_up, w_down):
-        x = jnp.take(emb, tokens.reshape(NMB * ROWS), axis=0).reshape(NMB, ROWS, D)
+        me = lax.axis_index("pp")
+        pair = jnp.where(me == FIRST, 0, jnp.where(me == 0, 1, me))
+        ids = lax.dynamic_slice_in_dim(tokens.reshape(NMB, ROWS), 2 * pair, 2, axis=0)
+        x = emb.at[ids.reshape(2 * ROWS)].get(mode="promise_in_bounds").reshape(2, ROWS, D)
         flag = jnp.broadcast_to(active.reshape(1, 1), (8, 128))
-        hbm = pl.BlockSpec(memory_space=pltpu.HBM)
-        vmem = pl.BlockSpec(memory_space=pltpu.VMEM)
-        dma, regular = pltpu.SemaphoreType.DMA, pltpu.SemaphoreType.REGULAR
-        token_loss = pl.pallas_call(
-            kernel,
-            out_shape=jax.ShapeDtypeStruct((NMB, ROWS), F32),
-            in_specs=[hbm, hbm, vmem, vmem, vmem, vmem] + [hbm] * 7 + [vmem, vmem],
-            out_specs=vmem,
-            scratch_shapes=[
-                pltpu.VMEM((NG, 3, D, CH), BF),
-                pltpu.VMEM((13, D, CH), BF),
-                pltpu.VMEM((2, NC, ROWS, CH), BF),
-                pltpu.VMEM((NC, ROWS, CH), BF),
-                pltpu.VMEM((NC, ROWS, CH), BF),
-                pltpu.VMEM((ROWS, D), BF),
-                pltpu.VMEM((NC, ROWS, CH), BF),
-                pltpu.VMEM((NC, ROWS, CH), BF),
-                pltpu.VMEM((NC, ROWS, CH), BF),
-                pltpu.VMEM((8, ROWS, 1024), BF),
-                pltpu.VMEM((2, NC, ROWS, CH), BF),
-                pltpu.VMEM((2, 3, NMB, ROWS), F32),
-                pltpu.VMEM((6, 8, ROWS), F32),
-                dma((NG,)), dma((13,)), dma((2, NC)), dma((2, NC)), dma((2, NC)), dma((2, NC)), regular, regular,
-                dma((3, NC)), dma((NC,)), dma((NC,)), dma((7,)), dma((2,)), dma((7,)), dma((6,)),
-            ],
-            compiler_params=pltpu.CompilerParams(vmem_limit_bytes=67043328, has_side_effects=True),
-        )(x, emb, g_final.reshape(1, D), targets.reshape(NMB, ROWS), g_attn.reshape(1, D), g_mlp.reshape(1, D),
+        token_loss, mean, _ = run_kernel(x, emb, g_final.reshape(1, D), targets.reshape(NMB, ROWS), g_attn.reshape(1, D), g_mlp.reshape(1, D),
           w_q.reshape(D, D), w_k.reshape(D, D), w_v.reshape(D, D), w_o.reshape(D, D),
           w_gate.reshape(D, FFN), w_up.reshape(D, FFN), w_down.reshape(FFN, D), rope_tables(), flag)
-        return token_loss.reshape(NMB, 2, 128), jnp.mean(token_loss, axis=1)
+        return token_loss, mean[0, :NMB]
 
     stack = P("pp")
     in_specs = (P("dp"), P("dp"), P(), P()) + (stack,) * 10

time: 1060 us -> 912 us (0.86)
  local copies, waits for them, and re-layouts: 99.2 us -> 13.1 us
  Pallas kernels: 939 us -> 897 us
  other arithmetic: 17.2 us -> 0.01 us
    gather x1, local copies, waits for them, and re-layouts: 95.7 us -> 6.72 us  [stage_program(): emb.at[ids.reshape(2 * ROWS)].get(mode='promise_in_bounds')]
    pallas_call x1, Pallas kernels: 939 us -> 897 us  [run_kernel(): pl.pallas_call(kernel, out_shape=(jax.ShapeDtypeStruct((NMB, 2, 128), F32...]
    select_n x2 -> x1, other arithmetic: 14.9 us -> 0.01 us  [stage_program(): emb.at[ids.reshape(2 * ROWS)].get(mode='promise_in_bounds')]
where the time goes in v1:
time: 912 us; the launch traced here: 911 us
  Pallas kernels  897 us (98%)
  local copies, waits for them, and re-layouts  13.1 us (1%)
    pallas_call x1, Pallas kernels, run_kernel(): pl.pallas_call(kernel, out_shape=(jax.ShapeDtypeStruct((NMB, 2, 128), F32...  897 us

profile of v1, /device:TPU:0, one launch (start us, length us, event | category | flops | bytes accessed | tf_op | source)
XLA Modules:
  0.0 911.2 jit_solution(14906074807078945740)
XLA Ops:
  1.3 0.6 broadcast_in_dim.9.flag
  1.9 1.3 reshape.77.gf
  3.2 0.7 copy.23
  3.9 1.3 copy.22
  5.3 6.7 gather_fusion
  12.0 896.7 %shard_map.158 = (f32[16,2,128]{2,1,0:T(2,128)}, f32[1,128]{1,0:T(1,128)}, bf16[8,2,256,2048]{3,2,1,0:T(8,128)(2,1)}) custom-call(bf16[2,256,2048]{2,1,0:T(8,128)(2,1)} %bitcast.31, bf16[49152,2048]{1,0:T(8,128)(2,1)} %emb.1, bf16[1,2048]{1,0:T(2,128)(2,1)} %reshape.77.gf, s32[16,256]{1,0:T(8,128)} %bitcast.36, bf16[1,2048]{1,0:T(2,128)(2,1)} %bitcast.40, ...), custom_call_target="tpu_custom_call" | custom-call | tf_op jit(solution)/shard_map/pallas_call | solution.py:654
  908.7 1.1 slice_bitcast_fusion
  909.8 1.3 copy.26
  (4 shorter events, 0.0 us)

commit v2 on v1

--- a/solution.py
+++ b/solution.py
@@ -25,7 +25,7 @@
 VOCAB = 49152
 CH = 512
 NC = D // CH
-NG = 3
+NG = 4
 BODIES = 17
 FIRST, LAST = 1, 6
 HG = 2048
@@ -56,11 +56,11 @@
 
 
 def norm_rows(src, g_ref, dst):
-    gains = [g_ref[:, CH * c:CH * (c + 1)].astype(F32) for c in range(NC)]
+    gains = [g_ref[0:1, CH * c:CH * (c + 1)].astype(F32) for c in range(NC)]
 
     def block(i, _):
-        r0 = pl.multiple_of(i * 128, 128)
-        for u in range(8):
+        r0 = pl.multiple_of(i * 256, 256)
+        for u in range(16):
             rows = pl.ds(r0 + 16 * u, 16)
             ss = None
             for c in range(NC):
@@ -74,7 +74,7 @@
                 dst[rows, CH * c:CH * (c + 1)] = (xv * inv * gains[c]).astype(BF)
         return 0
 
-    lax.fori_loop(0, ROWS // 128, block, 0)
+    lax.fori_loop(0, ROWS // 256, block, 0)
 
 
 def rope(y, tab, base):
@@ -90,7 +90,7 @@
 
 def attend_probs(q, k, ch, pair, seq, lo, causal):
     rows, cols = pl.ds(128 * seq, 128), pl.ds(128 * pair, 128)
-    qp, kp = q[ch, rows, cols], k[ch, rows, cols]
+    qp, kp = q[ch, rows, cols], k[rows, pl.ds(CH * (ch % 2) + 128 * pair, 128)]
     zero = jnp.zeros((128, 128), BF)
     both = jnp.concatenate([jnp.where(lo, kp, zero), jnp.where(lo, zero, kp)], axis=0)
     scores = dott(qp, both)
@@ -104,17 +104,18 @@
 
 def attend_values(q, v, ch, pair, seq, lo, probs):
     rows, cols = pl.ds(128 * seq, 128), pl.ds(128 * pair, 128)
-    vp = v[ch, rows, cols]
+    vp = v[rows, pl.ds(CH * (ch % 2) + 128 * pair, 128)]
     zero = jnp.zeros((128, 128), BF)
     both = jnp.concatenate([jnp.where(lo, vp, zero), jnp.where(lo, zero, vp)], axis=0)
     q[ch, rows, cols] = dotf(probs, both).astype(BF)
 
 
 def kernel(x_hbm, emb, gf, tgt, ga, gm, wq, wk, wv, wo, wg, wu, wd, tab, flag, out, out_mean, xbuf,
-           ring, res, xin, xfin, x1, h, q, k, v, a, xout, st, stf,
+           ring, res, xin, xfin, h, q, a, xout, st, stf,
            wsem, rsem, xsem, recv_sem, send_sem, send0_sem, free_sem, free0_sem,
            fsend_sem, frecv_sem, ffwd_sem, ssend_sem, srecv_sem, tsend_sem, trecv_sem, gsend_sem, grecv_sem):
     me = lax.axis_index("pp")
+    k, v = a.at[0], a.at[1]
     is_layer = jnp.logical_and(me >= FIRST, me <= LAST)
     is_head = jnp.logical_or(me == 0, me == 7)
     lane = lax.broadcasted_iota(jnp.int32, (128, 128), 1)
@@ -164,17 +165,17 @@
             load(down_tile(n, t), slot, t)
 
     def to_next(s, n):
-        return pltpu.make_async_remote_copy(xout.at[s, n], xin.at[s, n], send_sem.at[s, n], recv_sem.at[s, n],
+        return pltpu.make_async_remote_copy(xout.at[n], xin.at[s, n], send_sem.at[n], recv_sem.at[s, n],
                                             device_id={"pp": lax.rem(me + 1, 8)}, device_id_type=MESH)
 
     def to_zero(s, n):
-        return pltpu.make_async_remote_copy(xout.at[s, n], xin.at[s, n], send0_sem.at[s, n], recv_sem.at[s, n],
+        return pltpu.make_async_remote_copy(xout.at[n], xin.at[s, n], send0_sem.at[n], recv_sem.at[s, n],
                                             device_id={"pp": 0}, device_id_type=MESH)
 
     fin_targets = (7, 4, 2)
 
     def to_fin(i, s, n):
-        return pltpu.make_async_remote_copy(xout.at[s, n], xfin.at[n], fsend_sem.at[i, n], frecv_sem.at[n],
+        return pltpu.make_async_remote_copy(xout.at[n], xfin.at[n], fsend_sem.at[i, n], frecv_sem.at[n],
                                             device_id={"pp": fin_targets[i]}, device_id_type=MESH)
 
     def forward(n):
@@ -235,6 +236,9 @@
             mx = new
         return mx, sm, pk
 
+    def target_row(m):
+        return jnp.concatenate([tgt[m, 0:1, :], tgt[m, 1:2, :]], axis=1)
+
     def head_start():
         return (jnp.full((8, ROWS), -3e38, F32), jnp.zeros((8, ROWS), F32), jnp.zeros((8, ROWS), F32))
 
@@ -254,11 +258,13 @@
         def _():
             start_x(0, 0)
 
-        for i in range(3):
+        for i in range(2):
             start_qkv(i, i)
 
         @pl.when(me != FIRST)
         def _():
+            for i in range(2, NG):
+                start_qkv(i, i)
             load_res(cols_of(wo, 3), 0)
             for c in range(8):
                 load_res(cols_of(wu, 2 * c + 1), 1 + c)
@@ -287,66 +293,108 @@
             norm_rows(xin.at[s], ga, h)
             on = flag[0:1, 0:1] != 0
 
-            def qkv(i, prev):
+            def begin(*bodies):
+                for b in bodies:
+                    wait_group(slot_of(m, b))
+
+            def begin_res(*tiles):
+                @pl.when(first)
+                def _():
+                    for i in tiles:
+                        wait_res(i)
+
+            def start_body(b, slot):
+                if b < 4:
+                    start_qkv(b, slot)
+                elif b == 4:
+                    start_out(slot)
+                elif b < 13:
+                    start_ffn(b - 5, slot)
+                else:
+                    start_down(b - 13, slot)
+
+            def refill(b):
+                slot, later = slot_of(m, b), b + NG
+                if later < BODIES:
+                    start_body(later, slot)
+
+                    @pl.when(fresh)
+                    def _():
+                        if later == 4:
+                            load_res(cols_of(wo, 3), 0)
+                        elif later < 13:
+                            load_res(cols_of(wu, 2 * (later - 5) + 1), 1 + later - 5)
+                        else:
+                            load_res(down_tile(later - 13, 3), 9 + later - 13)
+                else:
+                    @pl.when(more)
+                    def _():
+                        start_body(later - BODIES, slot)
+
+            def qkv(i):
                 slot = slot_of(m, i)
-                wait_group(slot)
-                us = units if prev is not None else []
-                ps = [attend_probs(q, k, prev, p, sq, lo, causal) for p, sq in us]
+                us = units if i > 0 else []
+                ps = [attend_probs(q, k, i - 1, p, sq, lo, causal) for p, sq in us]
                 for j, dst in enumerate((q, k, v)):
                     r = dotf(h[...], ring[slot, j])
                     if j < 2:
                         r = rope(r, tab, 3 * j)
-                    dst[i] = r.astype(BF)
+                    if j == 0:
+                        q[i] = r.astype(BF)
+                    else:
+                        dst[:, CH * (i % 2):CH * (i % 2) + CH] = r.astype(BF)
                     for (p, sq), pr in zip(us, ps) if j == 1 else ():
-                        attend_values(q, v, prev, p, sq, lo, pr)
-                return slot
-
-            slot = qkv(0, None)
-            start_qkv(3, slot)
-
-            def qkv_static(i):
-                slot = qkv(i, i - 1)
-                if i == 1:
-                    start_out(slot)
-
-                    @pl.when(fresh)
+                        attend_values(q, v, i - 1, p, sq, lo, pr)
+
+            def ffn(c):
+                slot = slot_of(m, 5 + c)
+                for t in range(2):
+                    gate = dotf(h[...], ring[slot, t])
+                    up = dotf(h[...], ring[slot, 2] if t == 0 else res[1 + c])
+                    a[c, :, CH * t:CH * (t + 1)] = (gate * (1.0 / (1.0 + jnp.exp(-gate))) * up).astype(BF)
+
+            def down(n):
+                slot = slot_of(m, 13 + n)
+                acc = None
+                for t in range(4):
+                    w = ring.at[slot, t] if t < 3 else res.at[9 + n]
+                    for u in range(2):
+                        part = dotf(a[2 * t + u], w[1024 * u:1024 * (u + 1), :])
+                        acc = part if acc is None else acc + part
+                xo = xin[s, n]
+                xout[n] = jnp.where(on, (xo.astype(F32) + acc).astype(BF), xo)
+
+                @pl.when(jnp.logical_or(more, me != LAST))
+                def _():
+                    to_next(s, n).start()
+
+                @pl.when(me == LAST)
+                def _():
+                    @pl.when(more)
                     def _():
-                        load_res(cols_of(wo, 3), 0)
-                else:
-                    start_ffn(i - 2, slot)
-
-                    @pl.when(fresh)
+                        to_zero(s, n).start()
+
+                    @pl.when(jnp.logical_not(more))
                     def _():
-                        load_res(cols_of(wu, 2 * (i - 2) + 1), 1 + i - 2)
-
-            def qkv_loop(i, _):
-                slot = qkv(i, i - 1)
-
-                @pl.when(i == 1)
-                def _():
-                    start_out(slot)
-
-                    @pl.when(fresh)
-                    def _():
-                        load_res(cols_of(wo, 3), 0)
-
-                @pl.when(i > 1)
-                def _():
-                    start_ffn(i - 2, slot)
-
-                    @pl.when(fresh)
-                    def _():
-                        load_res(cols_of(wu, 2 * (i - 2) + 1), 1 + i - 2)
-                return 0
-
-            for i in range(1, 4):
-                qkv_static(i)
+                        for i in range(3):
+                            to_fin(i, s, n).start()
+
+            for i in (0, 2):
+                begin(i, i + 1)
+
+                @pl.when(jnp.logical_and(fresh, i == 0))
+                def _():
+                    for j in range(2, NG):
+                        start_qkv(j, j)
+
+                qkv(i)
+                refill(i)
+                qkv(i + 1)
+                refill(i + 1)
+
+            begin(4, 5)
+            begin_res(0, 1)
             slot = slot_of(m, 4)
-            wait_group(slot)
-
-            @pl.when(first)
-            def _():
-                wait_res(0)
 
             def out_tile(t):
                 return ring.at[slot, t] if t < 3 else res.at[0]
@@ -366,55 +414,26 @@
             for t in range(NC):
                 r = done[t] + dotf(q[3], out_tile(t)[CH * 3:, :])
                 xo = xin[s, t]
-                x1[t] = jnp.where(on, (xo.astype(F32) + r).astype(BF), xo)
-            start_ffn(2, slot)
-
-            @pl.when(fresh)
-            def _():
-                load_res(cols_of(wu, 2 * 2 + 1), 1 + 2)
-
-            @pl.when(jnp.logical_and(me != FIRST, m < NMB - 2))
-            def _():
-                pl.semaphore_signal(free_sem, 1, device_id={"pp": lax.rem(me + 7, 8)}, device_id_type=MESH)
-
-            norm_rows(x1, gm, h)
-
-            def ffn2(i, _):
-                for e in range(4):
-                    ffn(4 * i + e, 0)
+                xin[s, t] = jnp.where(on, (xo.astype(F32) + r).astype(BF), xo)
+            refill(4)
+            norm_rows(xin.at[s], gm, h)
+            ffn(0)
+            refill(5)
+
+            def ffn_pair(i, _):
+                c = 1 + 2 * i
+                begin(5 + c, 6 + c)
+                begin_res(1 + c, 2 + c)
+                ffn(c)
+                ffn(c + 1)
+                for e in range(3):
+                    @pl.when(i == e)
+                    def _():
+                        refill(6 + 2 * e)
+                        refill(7 + 2 * e)
                 return 0
 
-            def ffn(c, _):
-                slot = slot_of(m, 5 + c)
-                wait_group(slot)
-
-                @pl.when(first)
-                def _():
-                    wait_res(1 + c)
-
-                for t in range(2):
-                    gate = dotf(h[...], ring[slot, t])
-                    up = dotf(h[...], ring[slot, 2] if t == 0 else res[1 + c])
-                    a[c, :, CH * t:CH * (t + 1)] = (gate * (1.0 / (1.0 + jnp.exp(-gate))) * up).astype(BF)
-
-                @pl.when(c < 5)
-                def _():
-                    start_ffn(c + 3, slot)
-
-                    @pl.when(fresh)
-                    def _():
-                        load_res(cols_of(wu, 2 * (c + 3) + 1), 1 + c + 3)
-
-                @pl.when(c >= 5)
-                def _():
-                    start_down(c - 5, slot)
-
-                    @pl.when(fresh)
-                    def _():
-                        load_res(down_tile(c - 5, 3), 9 + c - 5)
-                return 0
-
-            lax.fori_loop(0, 2, ffn2, 0)
+            lax.fori_loop(0, 3, ffn_pair, 0)
 
             @pl.when(jnp.logical_and(m >= 2, jnp.logical_or(more, me != LAST)))
             def _():
@@ -424,60 +443,35 @@
                 def _():
                     pl.semaphore_wait(free0_sem, 1)
 
-            def down(n, _):
-                slot = slot_of(m, 13 + n)
-                wait_group(slot)
-
-                @pl.when(first)
-                def _():
-                    wait_res(9 + n)
-
-                @pl.when(m >= 2)
-                def _():
+            @pl.when(m >= 1)
+            def _():
+                for n in range(NC):
                     to_next(s, n).wait_send()
 
                     @pl.when(me == LAST)
                     def _():
                         to_zero(s, n).wait_send()
 
-                acc = None
-                for t in range(4):
-                    w = ring.at[slot, t] if t < 3 else res.at[9 + n]
-                    for u in range(2):
-                        part = dotf(a[2 * t + u], w[1024 * u:1024 * (u + 1), :])
-                        acc = part if acc is None else acc + part
-                xo = x1[n]
-                xout[s, n] = jnp.where(on, (xo.astype(F32) + acc).astype(BF), xo)
-
-                @pl.when(jnp.logical_or(more, me != LAST))
-                def _():
-                    to_next(s, n).start()
-
-                @pl.when(me == LAST)
-                def _():
-                    @pl.when(more)
-                    def _():
-                        to_zero(s, n).start()
-
-                    @pl.when(jnp.logical_not(more))
-                    def _():
-                        for i in range(3):
-                            to_fin(i, s, n).start()
-
-                if n == 0:
-                    start_down(3, slot)
-
-                    @pl.when(fresh)
-                    def _():
-                        load_res(down_tile(3, 3), 12)
-                else:
-                    @pl.when(more)
-                    def _():
-                        start_qkv(n - 1, slot)
-                return 0
-
-            for n in range(NC):
-                down(n, 0)
+            begin(12, 13)
+            begin_res(8, 9)
+            ffn(7)
+            refill(12)
+            down(0)
+            refill(13)
+            begin(14, 15)
+            begin_res(10, 11)
+            down(1)
+            refill(14)
+            down(2)
+            refill(15)
+            begin(16)
+            begin_res(12)
+            down(3)
+            refill(16)
+
+            @pl.when(jnp.logical_and(me != FIRST, m < NMB - 2))
+            def _():
+                pl.semaphore_signal(free_sem, 1, device_id={"pp": lax.rem(me + 7, 8)}, device_id_type=MESH)
             return 0
 
         lax.fori_loop(0, NMB, one, 0)
@@ -510,7 +504,7 @@
                 def _():
                     pl.semaphore_signal(free0_sem, 1, device_id={"pp": LAST}, device_id_type=MESH)
 
-            y = tgt[pl.ds(m, 1), :]
+            y = target_row(m)
 
             def group(g, carry):
                 slot = lax.rem(g, 3)
@@ -554,7 +548,7 @@
         @pl.when(me == LAST)
         def _():
             for n in range(NC):
-                xfin[n] = xout[(NMB - 1) % 2, n]
+                xfin[n] = xout[n]
 
         @pl.when(me != LAST)
         def _():
@@ -566,7 +560,7 @@
                     forward(n).start()
 
         norm_rows(xfin, gf, h)
-        y = tgt[NMB - 1:NMB, :]
+        y = target_row(NMB - 1)
 
         def group(g, carry):
             slot = lax.rem(g, 3)
@@ -619,15 +613,12 @@
     @pl.when(is_layer)
     def _():
         for n in range(NC):
-            to_next(0, n).wait_send()
-
             @pl.when(me != LAST)
             def _():
                 to_next(1, n).wait_send()
 
             @pl.when(me == LAST)
             def _():
-                to_zero(0, n).wait_send()
                 for i in range(3):
                     to_fin(i, 1, n).wait_send()
 
@@ -662,16 +653,13 @@
             pltpu.VMEM((13, D, CH), BF),
             pltpu.VMEM((2, NC, ROWS, CH), BF),
             pltpu.VMEM((NC, ROWS, CH), BF),
-            pltpu.VMEM((NC, ROWS, CH), BF),
             pltpu.VMEM((ROWS, D), BF),
             pltpu.VMEM((NC, ROWS, CH), BF),
+            pltpu.VMEM((8, ROWS, 1024), BF),
             pltpu.VMEM((NC, ROWS, CH), BF),
-            pltpu.VMEM((NC, ROWS, CH), BF),
-            pltpu.VMEM((8, ROWS, 1024), BF),
-            pltpu.VMEM((2, NC, ROWS, CH), BF),
             pltpu.VMEM((2, 3, NMB, ROWS), F32),
             pltpu.VMEM((6, 8, ROWS), F32),
-            dma((NG,)), dma((13,)), dma((2,)), dma((2, NC)), dma((2, NC)), dma((2, NC)), regular, regular,
+            dma((NG,)), dma((13,)), dma((2,)), dma((2, NC)), dma((NC,)), dma((NC,)), regular, regular,
             dma((3, NC)), dma((NC,)), dma((NC,)), dma((7,)), dma((2,)), dma((7,)), dma((6,)), dma(()), dma((8,)),
         ],
         compiler_params=pltpu.CompilerParams(vmem_limit_bytes=67043328, has_side_effects=True),
@@ -682,12 +670,11 @@
     def stage_program(tokens, targets, emb, g_final, active, g_attn, w_q, w_k, w_v, w_o, g_mlp, w_gate, w_up, w_down):
         me = lax.axis_index("pp")
         pair = jnp.where(me == FIRST, 0, jnp.where(me == 0, 1, me))
-        ids = lax.dynamic_slice_in_dim(tokens.reshape(NMB, ROWS), 2 * pair, 2, axis=0)
+        ids = lax.dynamic_slice_in_dim(tokens, 2 * pair, 2, axis=0)
         x = emb.at[ids.reshape(2 * ROWS)].get(mode="promise_in_bounds").reshape(2, ROWS, D)
-        flag = jnp.broadcast_to(active.reshape(1, 1), (8, 128))
-        token_loss, mean, _ = run_kernel(x, emb, g_final.reshape(1, D), targets.reshape(NMB, ROWS), g_attn.reshape(1, D), g_mlp.reshape(1, D),
+        token_loss, mean, _ = run_kernel(x, emb, jnp.broadcast_to(g_final, (8, D)), targets, g_attn.reshape(1, D), g_mlp.reshape(1, D),
           w_q.reshape(D, D), w_k.reshape(D, D), w_v.reshape(D, D), w_o.reshape(D, D),
-          w_gate.reshape(D, FFN), w_up.reshape(D, FFN), w_down.reshape(FFN, D), rope_tables(), flag)
+          w_gate.reshape(D, FFN), w_up.reshape(D, FFN), w_down.reshape(FFN, D), rope_tables(), active)
         return token_loss, mean[0, :NMB]
 
     stack = P("pp")

time: 912 us -> 885 us (0.970)
  Pallas kernels: 897 us -> 872 us
    pallas_call x1, Pallas kernels: 897 us -> 872 us  [run_kernel(): pl.pallas_call(kernel, out_shape=(jax.ShapeDtypeStruct((NMB, 2, 128), F32...]
where the time goes in v2:
time: 885 us
  Pallas kernels  872 us (99%)
  local copies, waits for them, and re-layouts  11.2 us (1%)
    pallas_call x1, Pallas kernels, run_kernel(): pl.pallas_call(kernel, out_shape=(jax.ShapeDtypeStruct((NMB, 2, 128), F32...  872 us

profile of v2, /device:TPU:0, one launch (start us, length us, event | category | flops | bytes accessed | tf_op | source)
XLA Modules:
  0.0 884.6 jit_solution(6195718671579914128)
XLA Ops:
  1.3 0.7 constant_dynamic-slice_fusion
  2.0 1.3 broadcast_in_dim.4.gf
  3.3 6.7 gather_fusion
  10.0 872.2 %shard_map.158 = (f32[16,2,128]{2,1,0:T(2,128)}, f32[1,128]{1,0:T(1,128)}, bf16[8,2,256,2048]{3,2,1,0:T(8,128)(2,1)}) custom-call(bf16[2,256,2048]{2,1,0:T(8,128)(2,1)} %bitcast.17, bf16[49152,2048]{1,0:T(8,128)(2,1)} %emb.1, bf16[8,2048]{1,0:T(8,128)(2,1)} %broadcast_in_dim.4.gf, s32[16,2,128]{2,1,0:T(2,128)} %tgt.1, bf16[1,2048]{1,0:T(2,128)(2,1)} %bitcast.22, ...), custom_call_target="tpu_custom_call" | custom-call | tf_op jit(solution)/shard_map/pallas_call | solution.py:645
  882.2 1.1 slice_bitcast_fusion
  883.3 1.3 copy.19
  (2 shorter events, 0.0 us)
